TPU v7x, 8 devices: a whole 2x2x1 slice. The times are simulated.
8 devices in a mesh: mp: 2 (over z, y), dp: 4 (over x, core).
Axes of the slice: x: 2, y: 2, z: 1, core: 2. Of those that a mesh axis runs over, the one named last changes fastest.
Arguments:
- a_mat: bfloat16 [2048, 98304], P(('mp', 'dp'))
- b_mat: bfloat16 [98304, 5632], P(('mp', 'dp'))
Outputs:
- output: bfloat16 [2048, 5632], P(('mp', 'dp'))
All inputs are finite; a program needn't handle non-finite values.
Results may differ from a plain program's by a relative error of at most 0.001.
Values are sent between devices in bfloat16 or wider.
A program may use at most 1 GiB of HBM per device.

v0:
```python
import jax
import jax.numpy as jnp
from jax import lax
from jax.sharding import PartitionSpec as P


def solution(mesh):
    mp_size = mesh.shape["mp"]
    dp_size = mesh.shape["dp"]

    def local_product(a_rows, b_rows):
        row_count = a_rows.shape[0]
        tok_piece = b_rows.shape[0]
        a_split = a_rows.reshape(row_count, mp_size, dp_size, tok_piece)
        a_cols = lax.all_to_all(a_split, "dp", 2, 0, tiled=True)
        a_cols = a_cols.reshape(row_count * dp_size, mp_size, tok_piece)
        b_group = lax.all_gather(b_rows, "mp", axis=0, tiled=False)
        part_sum = jnp.einsum("rit,itn->rn", a_cols, b_group, preferred_element_type=jnp.float32)
        row_sum = lax.psum_scatter(part_sum, "dp", scatter_dimension=0, tiled=True)
        return row_sum.astype(jnp.bfloat16)

    return jax.shard_map(
        local_product,
        mesh=mesh,
        in_specs=(P(("mp", "dp"), None), P(("mp", "dp"), None)),
        out_specs=P(("mp", "dp"), None),
        check_vma=False,
    )
```

profile of v0, /device:TPU:0, one launch (start us, length us, event | category | flops | bytes accessed | tf_op | source)
XLA Modules:
  0.0 3627.7 jit_solution(3349448331678032732)
XLA Ops:
  6.5 0.0 all-gather.3.cloned.1.call-start
  6.5 0.7 all-gather.3.cloned.1.call-update
  7.3 0.0 reduce-scatter.2.cloned.1.call-start
  7.3 64.6 %copy.5 = bf16[256,98304]{0,1:T(8,128)(2,1)} copy(bf16[256,98304]{1,0:T(8,128)(2,1)} %param.2) | data formatting | bytes 100663296 | tf_op args[0]
  71.9 58.6 %copy.6 = bf16[256,2,4,12288]{3,0,1,2:T(8,128)(2,1)} copy(bf16[256,2,4,12288]{0,3,2,1:T(8,128)(2,1)} %bitcast.11) | data formatting | bytes 100663296 | tf_op jit(solution)/shard_map/reshape | solution.py:14
  130.4 568.5 %all_to_all.15 = bf16[256,2,4,12288]{3,0,1,2:T(8,128)(2,1)} all-to-all(bf16[256,2,4,12288]{3,0,1,2:T(8,128)(2,1)} %copy.6), channel_id=1, replica_groups=mesh['mp'=2,'dp'=4] {'dp'}, dimensions={2} | all-to-all | bytes 100663296 | tf_op jit(solution)/shard_map/all_to_all | solution.py:15
  699.0 33.7 copy.7
  732.7 2402.5 %all-gather.3.cloned.1.call-done = bf16[24576,5632]{1,0:T(8,128)(2,1)} async-done(((bf16[12288,5632]{1,0:T(8,128)(2,1)}), bf16[24576,5632]{1,0:T(8,128)(2,1)}) %all-gather.3.cloned.1.call-update) | async-done | bytes 276824064 | tf_op jit(solution)/shard_map/all_gather | solution.py:17
  3135.2 324.5 %convolution_bitcast_fusion = f32[1024,5632]{1,0:T(8,128)} fusion(bf16[1024,2,12288]{2,0,1:T(8,128)(2,1)} %bitcast.12, bf16[2,12288,5632]{2,1,0:T(8,128)(2,1)} %bitcast.4), kind=kOutput, calls=%fused_computation | convolution fusion | flops 283467841536 | bytes 350224384 | tf_op jit(solution)/shard_map/rit,itn->rn/dot_general | solution.py:18
  3459.7 0.0 reduce-scatter.2.cloned.1.call-update
  3459.7 156.7 %reduce-scatter.2.cloned.1.call-done = f32[256,5632]{1,0:T(8,128)} async-done(((f32[1024,5632]{1,0:T(8,128)}), f32[256,5632]{1,0:T(8,128)}) %reduce-scatter.2.cloned.1.call-update) | async-done | bytes 5767184 | tf_op jit(solution)/shard_map/reduce_scatter | solution.py:19
  3616.4 4.5 convert_element_type.3
Async XLA Ops:
  6.5 3128.6 %all-gather.3.cloned.1.call-start = ((), (), s32[]{:S(2)}) async-start(), calls=%async_computation.3 | async-start | bytes 415236096 | tf_op jit(solution)/shard_map/all_gather | solution.py:17
  7.3 3609.2 %reduce-scatter.2.cloned.1.call-start = ((), (), s32[]{:S(2)}) async-start(), calls=%async_computation.2 | async-start | bytes 28835840 | tf_op jit(solution)/shard_map/reduce_scatter | solution.py:19
Sparse Core Ops, SparseCore 0:
  8.8 3126.2 all-gather.2
  3459.8 156.5 reduce-scatter.1
where the time goes:
time: 3630 us
  waiting for transfers between devices  2560 us (71%)
  blocking collectives  569 us (16%)
  matrix products  325 us (9%)
  local copies, waits for them, and re-layouts  157 us (4%)
    all_gather x1, waiting for transfers between devices, local_product(): b_group = lax.all_gather(b_rows, 'mp', axis=0, tiled=False)  2400 us
    all_to_all x1, blocking collectives, local_product(): a_cols = lax.all_to_all(a_split, 'dp', 2, 0, tiled=True)  569 us
    dot_general x1, matrix products, local_product(): jnp.einsum('rit,itn->rn', a_cols, b_group, preferred_element_type=jnp.flo...  325 us
    reduce_scatter x1, waiting for transfers between devices, local_product(): row_sum = lax.psum_scatter(part_sum, 'dp', scatter_dimension=0, tiled=True)  157 us
  transfers between devices with their start and end apart: 2, of which 2 were waited for; matrix products, arithmetic and copies ran while one was open for 4% of the time, Pallas kernels for 0%

commit v1 on v0

v1 whole, which is shorter than its diff:
```python
import jax
import jax.numpy as jnp
from jax import lax
from jax.experimental import pallas as pl
from jax.experimental.pallas import tpu as pltpu
from jax.sharding import PartitionSpec as P

MESH = pl.DeviceIdType.MESH
PEERS = ((1, 0, 0), (0, 1, 0), (1, 1, 0), (1, 0, 1), (0, 1, 1), (1, 1, 1), (0, 0, 1))
CHUNKS = 4
COLS = 512
PIECE = 2048
DEPTH = 4096
AHEAD = 1
LAG1 = 2
LAG2 = 2
SUMS1, SUMS2 = LAG1 + 2, LAG2 + 2
SLOTS1, SLOTS2 = 2 * LAG1 + 2, 2 * LAG2 + 2


def kernel(
    a_ref, b_ref, c_ref, g_ref,
    a_v, b_v, p_v, rd_v, s1_v, r1_v, s2_v, r2_v, o_v,
    a_send, a_recv, a_load, b_load, d_send, d_recv, s1_send, r1_recv, s2_send, r2_recv, o_sem,
):
    _, _, rows, k_dim = g_ref.shape
    half = 4 * rows
    blocks = b_ref.shape[1] // COLS
    pieces = k_dim // PIECE
    steps = CHUNKS * blocks

    y = lax.axis_index("mp")
    x = lax.axis_index("dp") // 2
    c = lax.axis_index("dp") % 2
    f = (1 - c) * x + c * y
    g = (1 - c) * y + c * x
    first = ((1 - c) * y + c * (1 - y), ((1 - c) * (1 - x) + c * x) * 2 + c)
    second = ((1 - c) * (1 - y) + c * y, ((1 - c) * x + c * (1 - x)) * 2 + c)
    sibling = (y, x * 2 + 1 - c)
    me = (y * 2 + x) * 2 + c
    my_pos = 4 * c + 2 * f + g

    def peer(i):
        dx, dy, dc = PEERS[i]
        px, py, pc = (x + dx) % 2, (y + dy) % 2, (c + dc) % 2
        pos = 4 * pc + (1 - pc) * (2 * px + py) + pc * (2 * py + px)
        return (py, px * 2 + pc), (py * 2 + px) * 2 + pc, pos

    def a_rows(j):
        return pl.ds(pl.multiple_of(j * rows, rows), rows)

    def a_copy(i, j, start, size):
        device, index, _ = peer(i)
        return pltpu.make_async_remote_copy(
            src_ref=a_ref.at[a_rows(j), pl.ds(pl.multiple_of(index * k_dim + start, 128), size)],
            dst_ref=g_ref.at[j, my_pos, :, pl.ds(pl.multiple_of(start, 128), size)],
            send_sem=a_send.at[j, i],
            recv_sem=a_recv.at[j, i],
            device_id=device,
            device_id_type=MESH,
        )

    def send_piece(u):
        for i in range(len(PEERS)):
            a_copy(i, u // pieces, (u % pieces) * PIECE, PIECE).start()

    def a_loads(j):
        copies = []
        for i in range(len(PEERS)):
            _, _, pos = peer(i)
            copies.append(pltpu.make_async_copy(
                g_ref.at[j, pos], a_v.at[pl.ds(pl.multiple_of(pos * rows, rows), rows), :], a_load.at[i]
            ))
        copies.append(pltpu.make_async_copy(
            a_ref.at[a_rows(j), pl.ds(pl.multiple_of(me * k_dim, 128), k_dim)],
            a_v.at[pl.ds(pl.multiple_of(my_pos * rows, rows), rows), :],
            a_load.at[len(PEERS)],
        ))
        return copies

    def b_copy(s):
        return pltpu.make_async_copy(
            b_ref.at[:, pl.ds(pl.multiple_of((s % blocks) * COLS, COLS), COLS)], b_v.at[s % 2], b_load.at[s % 2]
        )

    def d_copy(b):
        return pltpu.make_async_remote_copy(
            src_ref=p_v.at[b % 2, pl.ds(pl.multiple_of((1 - c) * half, half), half), :],
            dst_ref=rd_v.at[b % 2],
            send_sem=d_send.at[b % 2],
            recv_sem=d_recv.at[b % 2],
            device_id=sibling,
            device_id_type=MESH,
        )

    def first_copy(b):
        return pltpu.make_async_remote_copy(
            src_ref=s1_v.at[b % SUMS1, pl.ds(pl.multiple_of((1 - f) * 2 * rows, 2 * rows), 2 * rows), :],
            dst_ref=r1_v.at[b % SLOTS1],
            send_sem=s1_send.at[b % SUMS1],
            recv_sem=r1_recv.at[b % SLOTS1],
            device_id=first,
            device_id_type=MESH,
        )

    def second_copy(b):
        return pltpu.make_async_remote_copy(
            src_ref=s2_v.at[b % SUMS2, pl.ds(pl.multiple_of((1 - g) * rows, rows), rows), :],
            dst_ref=r2_v.at[b % SLOTS2],
            send_sem=s2_send.at[b % SUMS2],
            recv_sem=r2_recv.at[b % SLOTS2],
            device_id=second,
            device_id_type=MESH,
        )

    def out_copy(b):
        return pltpu.make_async_copy(
            o_v.at[b % 2],
            c_ref.at[a_rows(b // blocks), pl.ds(pl.multiple_of((b % blocks) * COLS, COLS), COLS)],
            o_sem.at[b % 2],
        )

    def valid(b):
        return jnp.logical_and(b >= 0, b < steps)

    b_copy(0).start()
    barrier = pltpu.get_barrier_semaphore()
    for i in range(len(PEERS)):
        pl.semaphore_signal(barrier, inc=1, device_id=peer(i)[0], device_id_type=MESH)
    pl.semaphore_wait(barrier, len(PEERS))

    @pl.loop(0, pieces + AHEAD)
    def _(u):
        send_piece(u)

    @pl.loop(0, steps + 3 + LAG1 + LAG2)
    def _(s):
        j, n = s // blocks, s % blocks

        @pl.when(s + 1 < steps)
        def _():
            b_copy(s + 1).start()

        @pl.when(valid(s - 1))
        def _():
            d_copy(s - 1).start()

        @pl.when(valid(s - 2))
        def _():
            first_copy(s - 2).start()

        @pl.when(valid(s - 3 - LAG1))
        def _():
            second_copy(s - 3 - LAG1).start()

        unit = (j + 1) * pieces + n // 2 + AHEAD

        @pl.when(jnp.logical_and(n % 2 == 0, unit < CHUNKS * pieces))
        def _():
            send_piece(unit)

        @pl.when(s < steps)
        def _():
            @pl.when(n == 0)
            def _():
                for i in range(len(PEERS)):
                    a_copy(i, j, 0, k_dim).wait_recv()
                loads = a_loads(j)
                for load in loads:
                    load.start()
                for load in loads:
                    load.wait()

            b_copy(s).wait()

            @pl.loop(0, k_dim // DEPTH)
            def _(k):
                part = pl.ds(pl.multiple_of(k * DEPTH, DEPTH), DEPTH)
                dot = jnp.dot(a_v[:, part], b_v[s % 2, part, :], preferred_element_type=jnp.float32)

                @pl.when(k == 0)
                def _():
                    p_v[s % 2] = dot

                @pl.when(k > 0)
                def _():
                    p_v[s % 2] += dot

        @pl.when(valid(s - 1))
        def _():
            b = s - 1
            d_copy(b).wait_recv()
            s1_v[b % SUMS1] = p_v[b % 2, pl.ds(pl.multiple_of(c * half, half), half), :] + rd_v[b % 2]
            d_copy(b).wait_send()

        @pl.when(valid(s - 2 - LAG1))
        def _():
            b = s - 2 - LAG1
            first_copy(b).wait_recv()
            kept = s1_v[b % SUMS1, pl.ds(pl.multiple_of(f * 2 * rows, 2 * rows), 2 * rows), :]
            s2_v[b % SUMS2] = kept + r1_v[b % SLOTS1]
            first_copy(b).wait_send()

        @pl.when(valid(s - 3 - LAG1 - LAG2))
        def _():
            b = s - 3 - LAG1 - LAG2

            @pl.when(b >= 2)
            def _():
                out_copy(b - 2).wait()

            second_copy(b).wait_recv()
            kept = s2_v[b % SUMS2, pl.ds(pl.multiple_of(g * rows, rows), rows), :]
            o_v[b % 2] = (kept + r2_v[b % SLOTS2]).astype(o_v.dtype)
            second_copy(b).wait_send()
            out_copy(b).start()

    out_copy(steps - 2).wait()
    out_copy(steps - 1).wait()

    @pl.loop(0, CHUNKS)
    def _(j):
        for i in range(len(PEERS)):
            a_copy(i, j, 0, k_dim).wait_send()


def solution(mesh):
    def local_product(a_rows, b_rows):
        row_count = a_rows.shape[0]
        k_dim, n_dim = b_rows.shape
        rows = row_count // CHUNKS
        f32, dma = jnp.float32, pltpu.SemaphoreType.DMA
        c_rows, _ = pl.pallas_call(
            kernel,
            name="exchange_matmul",
            out_shape=(
                jax.ShapeDtypeStruct((row_count, n_dim), jnp.bfloat16),
                jax.ShapeDtypeStruct((CHUNKS, 8, rows, k_dim), jnp.bfloat16),
            ),
            in_specs=[pl.BlockSpec(memory_space=pl.ANY)] * 2,
            out_specs=[pl.BlockSpec(memory_space=pl.ANY)] * 2,
            scratch_shapes=[
                pltpu.VMEM((8 * rows, k_dim), jnp.bfloat16),
                pltpu.VMEM((2, k_dim, COLS), jnp.bfloat16),
                pltpu.VMEM((2, 8 * rows, COLS), f32),
                pltpu.VMEM((2, 4 * rows, COLS), f32),
                pltpu.VMEM((SUMS1, 4 * rows, COLS), f32),
                pltpu.VMEM((SLOTS1, 2 * rows, COLS), f32),
                pltpu.VMEM((SUMS2, 2 * rows, COLS), f32),
                pltpu.VMEM((SLOTS2, rows, COLS), f32),
                pltpu.VMEM((2, rows, COLS), jnp.bfloat16),
                dma((CHUNKS, len(PEERS))),
                dma((CHUNKS, len(PEERS))),
                dma((len(PEERS) + 1,)),
                dma((2,)),
                dma((2,)),
                dma((2,)),
                dma((SUMS1,)),
                dma((SLOTS1,)),
                dma((SUMS2,)),
                dma((SLOTS2,)),
                dma((2,)),
            ],
            compiler_params=pltpu.CompilerParams(
                collective_id=0, has_side_effects=True, vmem_limit_bytes=62 * 1024 * 1024
            ),
            cost_estimate=pl.CostEstimate(
                flops=2 * 8 * row_count * k_dim * n_dim,
                bytes_accessed=2 * CHUNKS * k_dim * n_dim,
                transcendentals=0,
            ),
        )(a_rows, b_rows)
        return c_rows

    return jax.shard_map(
        local_product,
        mesh=mesh,
        in_specs=(P(("mp", "dp"), None), P(("mp", "dp"), None)),
        out_specs=P(("mp", "dp"), None),
        check_vma=False,
    )
```

time: 3630 us -> 775 us (0.21)
  waiting for transfers between devices: 2560 us -> 0 us
  Pallas kernels: 0 us -> 771 us
  blocking collectives: 569 us -> 0 us
  matrix products: 325 us -> 0 us
  local copies, waits for them, and re-layouts: 157 us -> 3.58 us
    all_gather x1 -> x0, waiting for transfers between devices: 2400 us -> none  [local_product(): b_group = lax.all_gather(b_rows, 'mp', axis=0, tiled=False)]
    pallas_call x0 -> x1, Pallas kernels: none -> 771 us  [local_product(): pl.pallas_call(kernel, name='exchange_matmul', out_shape=(jax.ShapeDtypeS...]
    all_to_all x1 -> x0, blocking collectives: 569 us -> none  [local_product(): a_cols = lax.all_to_all(a_split, 'dp', 2, 0, tiled=True)]
    dot_general x1 -> x0, matrix products: 325 us -> none  [local_product(): jnp.einsum('rit,itn->rn', a_cols, b_group, preferred_element_type=jnp.flo...]
    reduce_scatter x1 -> x0, waiting for transfers between devices: 157 us -> none  [local_product(): row_sum = lax.psum_scatter(part_sum, 'dp', scatter_dimension=0, tiled=True)]
    unnamed x1, local copies, waits for them, and re-layouts: 64.6 us -> 3.58 us
    reshape x1 -> x0, local copies, waits for them, and re-layouts: 58.6 us -> none  [local_product(): a_split = a_rows.reshape(row_count, mp_size, dp_size, tok_piece)]
  transfers between devices with their start and end apart: 2 -> 0, of which waited for: 2 -> 0; matrix products, arithmetic and copies ran while one was open for 4% -> 0% of each run, Pallas kernels for 0% -> 0%
where the time goes in v1:
time: 775 us
  Pallas kernels  771 us (99%)
    pallas_call x1, Pallas kernels, local_product(): pl.pallas_call(kernel, name='exchange_matmul', out_shape=(jax.ShapeDtypeS...  771 us

profile of v1, /device:TPU:0, one launch (start us, length us, event | category | flops | bytes accessed | tf_op | source)
XLA Modules:
  0.0 774.9 jit_solution(10712370275466265958)
XLA Ops:
  0.0 771.4 %exchange_matmul.1 = (bf16[256,5632]{1,0:T(8,128)(2,1)}, bf16[4,8,64,12288]{3,2,1,0:T(8,128)(2,1)}) custom-call(bf16[256,98304]{1,0:T(8,128)(2,1)} %a_ref.1, bf16[12288,5632]{1,0:T(8,128)(2,1)} %b_ref.1), custom_call_target="tpu_custom_call" | custom-call | flops 283467841536 | bytes 553648128 | tf_op jit(solution)/shard_map/exchange_matmul/pallas_call | solution.py:233
  771.4 3.6 copy.4

commit v2 on v1

--- a/solution.py
+++ b/solution.py
@@ -7,13 +7,12 @@
 
 MESH = pl.DeviceIdType.MESH
 PEERS = ((1, 0, 0), (0, 1, 0), (1, 1, 0), (1, 0, 1), (0, 1, 1), (1, 1, 1), (0, 0, 1))
-CHUNKS = 4
+CHUNKS = 8
 COLS = 512
 PIECE = 2048
-DEPTH = 4096
-AHEAD = 1
-LAG1 = 2
-LAG2 = 2
+AHEAD = 2
+LAG1 = 3
+LAG2 = 3
 SUMS1, SUMS2 = LAG1 + 2, LAG2 + 2
 SLOTS1, SLOTS2 = 2 * LAG1 + 2, 2 * LAG2 + 2
 
@@ -173,18 +172,7 @@
 
             b_copy(s).wait()
 
-            @pl.loop(0, k_dim // DEPTH)
-            def _(k):
-                part = pl.ds(pl.multiple_of(k * DEPTH, DEPTH), DEPTH)
-                dot = jnp.dot(a_v[:, part], b_v[s % 2, part, :], preferred_element_type=jnp.float32)
-
-                @pl.when(k == 0)
-                def _():
-                    p_v[s % 2] = dot
-
-                @pl.when(k > 0)
-                def _():
-                    p_v[s % 2] += dot
+            p_v[s % 2] = jnp.dot(a_v[...], b_v[s % 2], preferred_element_type=jnp.float32)
 
         @pl.when(valid(s - 1))
         def _():

time: 775 us -> 766 us (0.988)
  Pallas kernels: 771 us -> 761 us
    pallas_call x1, Pallas kernels: 771 us -> 761 us  [local_product(): pl.pallas_call(kernel, name='exchange_matmul', out_shape=(jax.ShapeDtypeS...]
where the time goes in v2:
time: 766 us; the launch traced here: 765 us
  Pallas kernels  761 us (99%)
    pallas_call x1, Pallas kernels, local_product(): pl.pallas_call(kernel, name='exchange_matmul', out_shape=(jax.ShapeDtypeS...  761 us

profile of v2, /device:TPU:0, one launch (start us, length us, event | category | flops | bytes accessed | tf_op | source)
XLA Modules:
  0.0 764.7 jit_solution(10102728454594497420)
XLA Ops:
  0.0 761.1 %exchange_matmul.1 = (bf16[256,5632]{1,0:T(8,128)(2,1)}, bf16[8,8,32,12288]{3,2,1,0:T(8,128)(2,1)}) custom-call(bf16[256,98304]{1,0:T(8,128)(2,1)} %a_ref.1, bf16[12288,5632]{1,0:T(8,128)(2,1)} %b_ref.1), custom_call_target="tpu_custom_call" | custom-call | flops 283467841536 | bytes 1107296256 | tf_op jit(solution)/shard_map/exchange_matmul/pallas_call | solution.py:221
  761.1 3.6 copy.4

commit v3 on v2

--- a/solution.py
+++ b/solution.py
@@ -1,3 +1,5 @@
+import functools
+
 import jax
 import jax.numpy as jnp
 from jax import lax
@@ -11,10 +13,12 @@
 COLS = 512
 PIECE = 2048
 AHEAD = 2
-LAG1 = 3
-LAG2 = 3
-SUMS1, SUMS2 = LAG1 + 2, LAG2 + 2
-SLOTS1, SLOTS2 = 2 * LAG1 + 2, 2 * LAG2 + 2
+HELD = 12
+BURST = 2
+LAG1 = 4
+LAG2 = 4
+SUMS1, SUMS2 = HELD + LAG1 + 3, BURST * (LAG2 + 2)
+SLOTS1, SLOTS2 = BURST * (2 * LAG1 + 2), BURST * (2 * LAG2 + 2)
 
 
 def kernel(
@@ -122,6 +126,16 @@
     def valid(b):
         return jnp.logical_and(b >= 0, b < steps)
 
+    catch_up = steps - max(blocks, HELD)
+
+    def sent(s):
+        extra = jnp.maximum(s - catch_up + 1, 0) * (BURST - 1)
+        return jnp.clip(jnp.minimum(s - 1, s - 1 - HELD + extra), 0, steps)
+
+    def each(low, high, body):
+        for i in range(BURST):
+            pl.when(low + i < high)(functools.partial(body, low + i))
+
     b_copy(0).start()
     barrier = pltpu.get_barrier_semaphore()
     for i in range(len(PEERS)):
@@ -144,13 +158,8 @@
         def _():
             d_copy(s - 1).start()
 
-        @pl.when(valid(s - 2))
-        def _():
-            first_copy(s - 2).start()
-
-        @pl.when(valid(s - 3 - LAG1))
-        def _():
-            second_copy(s - 3 - LAG1).start()
+        each(sent(s - 1), sent(s), lambda b: first_copy(b).start())
+        each(sent(s - 2 - LAG1), sent(s - 1 - LAG1), lambda b: second_copy(b).start())
 
         unit = (j + 1) * pieces + n // 2 + AHEAD
 
@@ -181,18 +190,13 @@
             s1_v[b % SUMS1] = p_v[b % 2, pl.ds(pl.multiple_of(c * half, half), half), :] + rd_v[b % 2]
             d_copy(b).wait_send()
 
-        @pl.when(valid(s - 2 - LAG1))
-        def _():
-            b = s - 2 - LAG1
+        def add_first(b):
             first_copy(b).wait_recv()
             kept = s1_v[b % SUMS1, pl.ds(pl.multiple_of(f * 2 * rows, 2 * rows), 2 * rows), :]
             s2_v[b % SUMS2] = kept + r1_v[b % SLOTS1]
             first_copy(b).wait_send()
 
-        @pl.when(valid(s - 3 - LAG1 - LAG2))
-        def _():
-            b = s - 3 - LAG1 - LAG2
-
+        def add_second(b):
             @pl.when(b >= 2)
             def _():
                 out_copy(b - 2).wait()
@@ -202,6 +206,9 @@
             o_v[b % 2] = (kept + r2_v[b % SLOTS2]).astype(o_v.dtype)
             second_copy(b).wait_send()
             out_copy(b).start()
+
+        each(sent(s - 1 - LAG1), sent(s - LAG1), add_first)
+        each(sent(s - 2 - LAG1 - LAG2), sent(s - 1 - LAG1 - LAG2), add_second)
 
     out_copy(steps - 2).wait()
     out_copy(steps - 1).wait()

time: 766 us -> 739 us (0.965)
  Pallas kernels: 761 us -> 733 us
    pallas_call x1, Pallas kernels: 761 us -> 733 us  [local_product(): pl.pallas_call(kernel, name='exchange_matmul', out_shape=(jax.ShapeDtypeS...]
where the time goes in v3:
time: 739 us; the launch traced here: 737 us
  Pallas kernels  733 us (99%)
    pallas_call x1, Pallas kernels, local_product(): pl.pallas_call(kernel, name='exchange_matmul', out_shape=(jax.ShapeDtypeS...  733 us

profile of v3, /device:TPU:0, one launch (start us, length us, event | category | flops | bytes accessed | tf_op | source)
XLA Modules:
  0.0 737.0 jit_solution(5834286894430715204)
XLA Ops:
  0.0 733.4 %exchange_matmul.1 = (bf16[256,5632]{1,0:T(8,128)(2,1)}, bf16[8,8,32,12288]{3,2,1,0:T(8,128)(2,1)}) custom-call(bf16[256,98304]{1,0:T(8,128)(2,1)} %a_ref.1, bf16[12288,5632]{1,0:T(8,128)(2,1)} %b_ref.1), custom_call_target="tpu_custom_call" | custom-call | flops 283467841536 | bytes 1107296256 | tf_op jit(solution)/shard_map/exchange_matmul/pallas_call | solution.py:228
  733.4 3.6 copy.4

commit v4 on v3

--- a/solution.py
+++ b/solution.py
@@ -13,9 +13,9 @@
 COLS = 512
 PIECE = 2048
 AHEAD = 2
-HELD = 12
+HELD = 16
 BURST = 2
-LAG1 = 4
+LAG1 = 5
 LAG2 = 4
 SUMS1, SUMS2 = HELD + LAG1 + 3, BURST * (LAG2 + 2)
 SLOTS1, SLOTS2 = BURST * (2 * LAG1 + 2), BURST * (2 * LAG2 + 2)
@@ -23,8 +23,8 @@
 
 def kernel(
     a_ref, b_ref, c_ref, g_ref,
-    a_v, b_v, p_v, rd_v, s1_v, r1_v, s2_v, r2_v, o_v,
-    a_send, a_recv, a_load, b_load, d_send, d_recv, s1_send, r1_recv, s2_send, r2_recv, o_sem,
+    a_v, b_v, p_v, rd_v, s1_v, r1_v, s2_v, r2_v,
+    a_send, a_recv, a_load, b_load, d_send, d_recv, s1_send, r1_recv, s2_send, r2_recv,
 ):
     _, _, rows, k_dim = g_ref.shape
     half = 4 * rows
@@ -116,17 +116,10 @@
             device_id_type=MESH,
         )
 
-    def out_copy(b):
-        return pltpu.make_async_copy(
-            o_v.at[b % 2],
-            c_ref.at[a_rows(b // blocks), pl.ds(pl.multiple_of((b % blocks) * COLS, COLS), COLS)],
-            o_sem.at[b % 2],
-        )
-
     def valid(b):
         return jnp.logical_and(b >= 0, b < steps)
 
-    catch_up = steps - max(blocks, HELD)
+    catch_up = steps - HELD
 
     def sent(s):
         extra = jnp.maximum(s - catch_up + 1, 0) * (BURST - 1)
@@ -197,21 +190,14 @@
             first_copy(b).wait_send()
 
         def add_second(b):
-            @pl.when(b >= 2)
-            def _():
-                out_copy(b - 2).wait()
-
             second_copy(b).wait_recv()
             kept = s2_v[b % SUMS2, pl.ds(pl.multiple_of(g * rows, rows), rows), :]
-            o_v[b % 2] = (kept + r2_v[b % SLOTS2]).astype(o_v.dtype)
+            part = pl.ds(pl.multiple_of((b % blocks) * COLS, COLS), COLS)
+            c_ref[a_rows(b // blocks), part] = (kept + r2_v[b % SLOTS2]).astype(c_ref.dtype)
             second_copy(b).wait_send()
-            out_copy(b).start()
 
         each(sent(s - 1 - LAG1), sent(s - LAG1), add_first)
         each(sent(s - 2 - LAG1 - LAG2), sent(s - 1 - LAG1 - LAG2), add_second)
-
-    out_copy(steps - 2).wait()
-    out_copy(steps - 1).wait()
 
     @pl.loop(0, CHUNKS)
     def _(j):
@@ -229,11 +215,11 @@
             kernel,
             name="exchange_matmul",
             out_shape=(
-                jax.ShapeDtypeStruct((row_count, n_dim), jnp.bfloat16),
+                pltpu.VMEM((row_count, n_dim), jnp.bfloat16),
                 jax.ShapeDtypeStruct((CHUNKS, 8, rows, k_dim), jnp.bfloat16),
             ),
             in_specs=[pl.BlockSpec(memory_space=pl.ANY)] * 2,
-            out_specs=[pl.BlockSpec(memory_space=pl.ANY)] * 2,
+            out_specs=[pl.BlockSpec(memory_space=pltpu.VMEM), pl.BlockSpec(memory_space=pl.ANY)],
             scratch_shapes=[
                 pltpu.VMEM((8 * rows, k_dim), jnp.bfloat16),
                 pltpu.VMEM((2, k_dim, COLS), jnp.bfloat16),
@@ -243,7 +229,6 @@
                 pltpu.VMEM((SLOTS1, 2 * rows, COLS), f32),
                 pltpu.VMEM((SUMS2, 2 * rows, COLS), f32),
                 pltpu.VMEM((SLOTS2, rows, COLS), f32),
-                pltpu.VMEM((2, rows, COLS), jnp.bfloat16),
                 dma((CHUNKS, len(PEERS))),
                 dma((CHUNKS, len(PEERS))),
                 dma((len(PEERS) + 1,)),
@@ -254,10 +239,9 @@
                 dma((SLOTS1,)),
                 dma((SUMS2,)),
                 dma((SLOTS2,)),
-                dma((2,)),
             ],
             compiler_params=pltpu.CompilerParams(
-                collective_id=0, has_side_effects=True, vmem_limit_bytes=62 * 1024 * 1024
+                collective_id=0, has_side_effects=True, vmem_limit_bytes=56 * 1024 * 1024
             ),
             cost_estimate=pl.CostEstimate(
                 flops=2 * 8 * row_count * k_dim * n_dim,

time: 739 us -> 737 us (level)
  no operation moved by 1% of the time
where the time goes in v4:
time: 737 us; the launch traced here: 736 us
  Pallas kernels  734 us (100%)
    pallas_call x1, Pallas kernels, local_product(): pl.pallas_call(kernel, name='exchange_matmul', out_shape=(pltpu.VMEM((row...  734 us

profile of v4, /device:TPU:0, one launch (start us, length us, event | category | flops | bytes accessed | tf_op | source)
XLA Modules:
  0.0 735.8 jit_solution(3825355169054202130)
XLA Ops:
  0.0 734.2 %exchange_matmul.1 = (bf16[256,5632]{1,0:T(8,128)(2,1)S(1)}, bf16[8,8,32,12288]{3,2,1,0:T(8,128)(2,1)}) custom-call(bf16[256,98304]{1,0:T(8,128)(2,1)} %a_ref.1, bf16[12288,5632]{1,0:T(8,128)(2,1)} %b_ref.1), custom_call_target="tpu_custom_call" | custom-call | flops 283467841536 | bytes 1107296256 | tf_op jit(solution)/shard_map/exchange_matmul/pallas_call | solution.py:214
  734.2 1.6 copy.4

commit v5 on v4

--- a/solution.py
+++ b/solution.py
@@ -13,20 +13,24 @@
 COLS = 512
 PIECE = 2048
 AHEAD = 2
-HELD = 16
+HELD = 12
 BURST = 2
-LAG1 = 5
-LAG2 = 4
+LAG1 = 4
+LAG2 = 3
 SUMS1, SUMS2 = HELD + LAG1 + 3, BURST * (LAG2 + 2)
 SLOTS1, SLOTS2 = BURST * (2 * LAG1 + 2), BURST * (2 * LAG2 + 2)
+SENDS1, SENDS2 = BURST * (LAG1 + 1), BURST * (LAG2 + 1)
+ARRIVING = 3
+BUFFERS = 3
 
 
 def kernel(
     a_ref, b_ref, c_ref, g_ref,
-    a_v, b_v, p_v, rd_v, s1_v, r1_v, s2_v, r2_v,
-    a_send, a_recv, a_load, b_load, d_send, d_recv, s1_send, r1_recv, s2_send, r2_recv,
+    first_v, a_v, b_v, p_v, rd_v, s1_v, r1_v, s2_v, r2_v,
+    first_load, a_send, a_recv, a_load, b_load, d_send, d_recv, s1_send, r1_recv, s2_send, r2_recv,
 ):
-    _, _, rows, k_dim = g_ref.shape
+    _, all_rows, k_dim = g_ref.shape
+    rows = all_rows // CHUNKS
     half = 4 * rows
     blocks = b_ref.shape[1] // COLS
     pieces = k_dim // PIECE
@@ -52,16 +56,31 @@
     def a_rows(j):
         return pl.ds(pl.multiple_of(j * rows, rows), rows)
 
-    def a_copy(i, j, start, size):
-        device, index, _ = peer(i)
-        return pltpu.make_async_remote_copy(
-            src_ref=a_ref.at[a_rows(j), pl.ds(pl.multiple_of(index * k_dim + start, 128), size)],
-            dst_ref=g_ref.at[j, my_pos, :, pl.ds(pl.multiple_of(start, 128), size)],
-            send_sem=a_send.at[j, i],
-            recv_sem=a_recv.at[j, i],
-            device_id=device,
-            device_id_type=MESH,
-        )
+    def a_columns(i, start, size):
+        return pl.ds(pl.multiple_of(peer(i)[1] * k_dim + start, 128), size)
+
+    def a_copy(i, j, start, size, src_ref=None):
+        return pltpu.make_async_remote_copy(
+            src_ref=a_ref.at[a_rows(j), a_columns(i, start, size)] if src_ref is None else src_ref,
+            dst_ref=g_ref.at[my_pos, a_rows(j), pl.ds(pl.multiple_of(start, 128), size)],
+            send_sem=a_send.at[i],
+            recv_sem=a_recv.at[j % ARRIVING, i],
+            device_id=peer(i)[0],
+            device_id_type=MESH,
+        )
+
+    def a_sent(i):
+        return pltpu.make_async_remote_copy(
+            src_ref=a_ref.at[:, a_columns(i, 0, k_dim)],
+            dst_ref=g_ref.at[my_pos],
+            send_sem=a_send.at[i],
+            recv_sem=a_recv.at[0, i],
+            device_id=peer(i)[0],
+            device_id_type=MESH,
+        )
+
+    def first_piece(i):
+        return pltpu.make_async_copy(a_ref.at[a_rows(0), a_columns(i, 0, PIECE)], first_v.at[i], first_load.at[i])
 
     def send_piece(u):
         for i in range(len(PEERS)):
@@ -72,7 +91,7 @@
         for i in range(len(PEERS)):
             _, _, pos = peer(i)
             copies.append(pltpu.make_async_copy(
-                g_ref.at[j, pos], a_v.at[pl.ds(pl.multiple_of(pos * rows, rows), rows), :], a_load.at[i]
+                g_ref.at[pos, a_rows(j)], a_v.at[pl.ds(pl.multiple_of(pos * rows, rows), rows), :], a_load.at[i]
             ))
         copies.append(pltpu.make_async_copy(
             a_ref.at[a_rows(j), pl.ds(pl.multiple_of(me * k_dim, 128), k_dim)],
@@ -83,7 +102,7 @@
 
     def b_copy(s):
         return pltpu.make_async_copy(
-            b_ref.at[:, pl.ds(pl.multiple_of((s % blocks) * COLS, COLS), COLS)], b_v.at[s % 2], b_load.at[s % 2]
+            b_ref.at[:, pl.ds(pl.multiple_of((s % blocks) * COLS, COLS), COLS)], b_v.at[s % BUFFERS], b_load.at[s % BUFFERS]
         )
 
     def d_copy(b):
@@ -100,7 +119,7 @@
         return pltpu.make_async_remote_copy(
             src_ref=s1_v.at[b % SUMS1, pl.ds(pl.multiple_of((1 - f) * 2 * rows, 2 * rows), 2 * rows), :],
             dst_ref=r1_v.at[b % SLOTS1],
-            send_sem=s1_send.at[b % SUMS1],
+            send_sem=s1_send.at[b % SENDS1],
             recv_sem=r1_recv.at[b % SLOTS1],
             device_id=first,
             device_id_type=MESH,
@@ -110,7 +129,7 @@
         return pltpu.make_async_remote_copy(
             src_ref=s2_v.at[b % SUMS2, pl.ds(pl.multiple_of((1 - g) * rows, rows), rows), :],
             dst_ref=r2_v.at[b % SLOTS2],
-            send_sem=s2_send.at[b % SUMS2],
+            send_sem=s2_send.at[b % SENDS2],
             recv_sem=r2_recv.at[b % SLOTS2],
             device_id=second,
             device_id_type=MESH,
@@ -129,13 +148,20 @@
         for i in range(BURST):
             pl.when(low + i < high)(functools.partial(body, low + i))
 
-    b_copy(0).start()
     barrier = pltpu.get_barrier_semaphore()
     for i in range(len(PEERS)):
         pl.semaphore_signal(barrier, inc=1, device_id=peer(i)[0], device_id_type=MESH)
+    for i in range(len(PEERS)):
+        first_piece(i).start()
+    for s in range(BUFFERS - 1):
+        b_copy(s).start()
     pl.semaphore_wait(barrier, len(PEERS))
 
-    @pl.loop(0, pieces + AHEAD)
+    for i in range(len(PEERS)):
+        first_piece(i).wait()
+        a_copy(i, 0, 0, PIECE, first_v.at[i]).start()
+
+    @pl.loop(1, pieces + AHEAD)
     def _(u):
         send_piece(u)
 
@@ -143,9 +169,9 @@
     def _(s):
         j, n = s // blocks, s % blocks
 
-        @pl.when(s + 1 < steps)
-        def _():
-            b_copy(s + 1).start()
+        @pl.when(s + BUFFERS - 1 < steps)
+        def _():
+            b_copy(s + BUFFERS - 1).start()
 
         @pl.when(valid(s - 1))
         def _():
@@ -174,7 +200,7 @@
 
             b_copy(s).wait()
 
-            p_v[s % 2] = jnp.dot(a_v[...], b_v[s % 2], preferred_element_type=jnp.float32)
+            p_v[s % 2] = jnp.dot(a_v[...], b_v[s % BUFFERS], preferred_element_type=jnp.float32)
 
         @pl.when(valid(s - 1))
         def _():
@@ -199,10 +225,8 @@
         each(sent(s - 1 - LAG1), sent(s - LAG1), add_first)
         each(sent(s - 2 - LAG1 - LAG2), sent(s - 1 - LAG1 - LAG2), add_second)
 
-    @pl.loop(0, CHUNKS)
-    def _(j):
-        for i in range(len(PEERS)):
-            a_copy(i, j, 0, k_dim).wait_send()
+    for i in range(len(PEERS)):
+        a_sent(i).wait_send()
 
 
 def solution(mesh):
@@ -216,32 +240,34 @@
             name="exchange_matmul",
             out_shape=(
                 pltpu.VMEM((row_count, n_dim), jnp.bfloat16),
-                jax.ShapeDtypeStruct((CHUNKS, 8, rows, k_dim), jnp.bfloat16),
+                jax.ShapeDtypeStruct((8, row_count, k_dim), jnp.bfloat16),
             ),
             in_specs=[pl.BlockSpec(memory_space=pl.ANY)] * 2,
             out_specs=[pl.BlockSpec(memory_space=pltpu.VMEM), pl.BlockSpec(memory_space=pl.ANY)],
             scratch_shapes=[
+                pltpu.VMEM((len(PEERS), rows, PIECE), jnp.bfloat16),
                 pltpu.VMEM((8 * rows, k_dim), jnp.bfloat16),
-                pltpu.VMEM((2, k_dim, COLS), jnp.bfloat16),
+                pltpu.VMEM((BUFFERS, k_dim, COLS), jnp.bfloat16),
                 pltpu.VMEM((2, 8 * rows, COLS), f32),
                 pltpu.VMEM((2, 4 * rows, COLS), f32),
                 pltpu.VMEM((SUMS1, 4 * rows, COLS), f32),
                 pltpu.VMEM((SLOTS1, 2 * rows, COLS), f32),
                 pltpu.VMEM((SUMS2, 2 * rows, COLS), f32),
                 pltpu.VMEM((SLOTS2, rows, COLS), f32),
-                dma((CHUNKS, len(PEERS))),
-                dma((CHUNKS, len(PEERS))),
+                dma((len(PEERS),)),
+                dma((len(PEERS),)),
+                dma((ARRIVING, len(PEERS))),
                 dma((len(PEERS) + 1,)),
+                dma((BUFFERS,)),
                 dma((2,)),
                 dma((2,)),
-                dma((2,)),
-                dma((SUMS1,)),
+                dma((SENDS1,)),
                 dma((SLOTS1,)),
-                dma((SUMS2,)),
+                dma((SENDS2,)),
                 dma((SLOTS2,)),
             ],
             compiler_params=pltpu.CompilerParams(
-                collective_id=0, has_side_effects=True, vmem_limit_bytes=56 * 1024 * 1024
+                collective_id=0, has_side_effects=True, vmem_limit_bytes=59 * 1024 * 1024
             ),
             cost_estimate=pl.CostEstimate(
                 flops=2 * 8 * row_count * k_dim * n_dim,

time: 737 us -> 734 us (level)
  no operation moved by 1% of the time
where the time goes in v5:
time: 734 us
  Pallas kernels  733 us (100%)
    pallas_call x1, Pallas kernels, local_product(): pl.pallas_call(kernel, name='exchange_matmul', out_shape=(pltpu.VMEM((row...  733 us

profile of v5, /device:TPU:0, one launch (start us, length us, event | category | flops | bytes accessed | tf_op | source)
XLA Modules:
  0.0 734.1 jit_solution(7512508458212289445)
XLA Ops:
  0.0 732.5 %exchange_matmul.1 = (bf16[256,5632]{1,0:T(8,128)(2,1)S(1)}, bf16[8,256,12288]{2,1,0:T(8,128)(2,1)}) custom-call(bf16[256,98304]{1,0:T(8,128)(2,1)} %a_ref.1, bf16[12288,5632]{1,0:T(8,128)(2,1)} %b_ref.1), custom_call_target="tpu_custom_call" | custom-call | flops 283467841536 | bytes 1107296256 | tf_op jit(solution)/shard_map/exchange_matmul/pallas_call | solution.py:238
  732.5 1.6 copy.4

commit v6 on v5

--- a/solution.py
+++ b/solution.py
@@ -17,7 +17,8 @@
 BURST = 2
 LAG1 = 4
 LAG2 = 3
-SUMS1, SUMS2 = HELD + LAG1 + 3, BURST * (LAG2 + 2)
+HELD2 = 4
+SUMS1, SUMS2 = HELD + LAG1 + 3, BURST * (HELD2 + LAG2 + 2)
 SLOTS1, SLOTS2 = BURST * (2 * LAG1 + 2), BURST * (2 * LAG2 + 2)
 SENDS1, SENDS2 = BURST * (LAG1 + 1), BURST * (LAG2 + 1)
 ARRIVING = 3
@@ -27,7 +28,7 @@
 def kernel(
     a_ref, b_ref, c_ref, g_ref,
     first_v, a_v, b_v, p_v, rd_v, s1_v, r1_v, s2_v, r2_v,
-    first_load, a_send, a_recv, a_load, b_load, d_send, d_recv, s1_send, r1_recv, s2_send, r2_recv,
+    a_send, a_recv, a_load, b_load, d_send, d_recv, s1_send, r1_recv, s2_send, r2_recv,
 ):
     _, all_rows, k_dim = g_ref.shape
     rows = all_rows // CHUNKS
@@ -80,7 +81,7 @@
         )
 
     def first_piece(i):
-        return pltpu.make_async_copy(a_ref.at[a_rows(0), a_columns(i, 0, PIECE)], first_v.at[i], first_load.at[i])
+        return pltpu.make_async_copy(a_ref.at[a_rows(0), a_columns(i, 0, PIECE)], first_v.at[i], a_load.at[i])
 
     def send_piece(u):
         for i in range(len(PEERS)):
@@ -165,7 +166,7 @@
     def _(u):
         send_piece(u)
 
-    @pl.loop(0, steps + 3 + LAG1 + LAG2)
+    @pl.loop(0, steps + 3 + LAG1 + HELD2 + LAG2)
     def _(s):
         j, n = s // blocks, s % blocks
 
@@ -178,7 +179,7 @@
             d_copy(s - 1).start()
 
         each(sent(s - 1), sent(s), lambda b: first_copy(b).start())
-        each(sent(s - 2 - LAG1), sent(s - 1 - LAG1), lambda b: second_copy(b).start())
+        each(sent(s - 2 - LAG1 - HELD2), sent(s - 1 - LAG1 - HELD2), lambda b: second_copy(b).start())
 
         unit = (j + 1) * pieces + n // 2 + AHEAD
 
@@ -223,7 +224,7 @@
             second_copy(b).wait_send()
 
         each(sent(s - 1 - LAG1), sent(s - LAG1), add_first)
-        each(sent(s - 2 - LAG1 - LAG2), sent(s - 1 - LAG1 - LAG2), add_second)
+        each(sent(s - 2 - LAG1 - HELD2 - LAG2), sent(s - 1 - LAG1 - HELD2 - LAG2), add_second)
 
     for i in range(len(PEERS)):
         a_sent(i).wait_send()
@@ -255,7 +256,6 @@
                 pltpu.VMEM((SUMS2, 2 * rows, COLS), f32),
                 pltpu.VMEM((SLOTS2, rows, COLS), f32),
                 dma((len(PEERS),)),
-                dma((len(PEERS),)),
                 dma((ARRIVING, len(PEERS))),
                 dma((len(PEERS) + 1,)),
                 dma((BUFFERS,)),

time: 734 us -> 734 us (level)
  no operation moved by 1% of the time
where the time goes in v6:
time: 734 us
  Pallas kernels  732 us (100%)
    pallas_call x1, Pallas kernels, local_product(): pl.pallas_call(kernel, name='exchange_matmul', out_shape=(pltpu.VMEM((row...  732 us

profile of v6, /device:TPU:0, one launch (start us, length us, event | category | flops | bytes accessed | tf_op | source)
XLA Modules:
  0.0 733.8 jit_solution(6498616278300883483)
XLA Ops:
  0.0 732.2 %exchange_matmul.1 = (bf16[256,5632]{1,0:T(8,128)(2,1)S(1)}, bf16[8,256,12288]{2,1,0:T(8,128)(2,1)}) custom-call(bf16[256,98304]{1,0:T(8,128)(2,1)} %a_ref.1, bf16[12288,5632]{1,0:T(8,128)(2,1)} %b_ref.1), custom_call_target="tpu_custom_call" | custom-call | flops 283467841536 | bytes 1107296256 | tf_op jit(solution)/shard_map/exchange_matmul/pallas_call | solution.py:239
  732.3 1.6 copy.4

commit v7 on v6

--- a/solution.py
+++ b/solution.py
@@ -65,7 +65,7 @@
             src_ref=a_ref.at[a_rows(j), a_columns(i, start, size)] if src_ref is None else src_ref,
             dst_ref=g_ref.at[my_pos, a_rows(j), pl.ds(pl.multiple_of(start, 128), size)],
             send_sem=a_send.at[i],
-            recv_sem=a_recv.at[j % ARRIVING, i],
+            recv_sem=a_recv.at[j % ARRIVING],
             device_id=peer(i)[0],
             device_id_type=MESH,
         )
@@ -75,13 +75,13 @@
             src_ref=a_ref.at[:, a_columns(i, 0, k_dim)],
             dst_ref=g_ref.at[my_pos],
             send_sem=a_send.at[i],
-            recv_sem=a_recv.at[0, i],
+            recv_sem=a_recv.at[0],
             device_id=peer(i)[0],
             device_id_type=MESH,
         )
 
     def first_piece(i):
-        return pltpu.make_async_copy(a_ref.at[a_rows(0), a_columns(i, 0, PIECE)], first_v.at[i], a_load.at[i])
+        return pltpu.make_async_copy(a_ref.at[a_rows(0), a_columns(i, 0, PIECE)], first_v.at[i], a_load)
 
     def send_piece(u):
         for i in range(len(PEERS)):
@@ -92,12 +92,12 @@
         for i in range(len(PEERS)):
             _, _, pos = peer(i)
             copies.append(pltpu.make_async_copy(
-                g_ref.at[pos, a_rows(j)], a_v.at[pl.ds(pl.multiple_of(pos * rows, rows), rows), :], a_load.at[i]
+                g_ref.at[pos, a_rows(j)], a_v.at[pl.ds(pl.multiple_of(pos * rows, rows), rows), :], a_load
             ))
         copies.append(pltpu.make_async_copy(
             a_ref.at[a_rows(j), pl.ds(pl.multiple_of(me * k_dim, 128), k_dim)],
             a_v.at[pl.ds(pl.multiple_of(my_pos * rows, rows), rows), :],
-            a_load.at[len(PEERS)],
+            a_load,
         ))
         return copies
 
@@ -158,8 +158,8 @@
         b_copy(s).start()
     pl.semaphore_wait(barrier, len(PEERS))
 
-    for i in range(len(PEERS)):
-        first_piece(i).wait()
+    pltpu.make_async_copy(g_ref.at[pl.ds(0, len(PEERS)), a_rows(0), pl.ds(0, PIECE)], first_v, a_load).wait()
+    for i in range(len(PEERS)):
         a_copy(i, 0, 0, PIECE, first_v.at[i]).start()
 
     @pl.loop(1, pieces + AHEAD)
@@ -191,13 +191,11 @@
         def _():
             @pl.when(n == 0)
             def _():
-                for i in range(len(PEERS)):
-                    a_copy(i, j, 0, k_dim).wait_recv()
-                loads = a_loads(j)
-                for load in loads:
+                arrived = g_ref.at[pl.ds(0, len(PEERS)), a_rows(j)]
+                pltpu.make_async_copy(arrived, arrived, a_recv.at[j % ARRIVING]).wait()
+                for load in a_loads(j):
                     load.start()
-                for load in loads:
-                    load.wait()
+                pltpu.make_async_copy(a_ref.at[:, pl.ds(0, k_dim)], a_v, a_load).wait()
 
             b_copy(s).wait()
 
@@ -256,8 +254,8 @@
                 pltpu.VMEM((SUMS2, 2 * rows, COLS), f32),
                 pltpu.VMEM((SLOTS2, rows, COLS), f32),
                 dma((len(PEERS),)),
-                dma((ARRIVING, len(PEERS))),
-                dma((len(PEERS) + 1,)),
+                dma((ARRIVING,)),
+                dma(()),
                 dma((BUFFERS,)),
                 dma((2,)),
                 dma((2,)),

time: 734 us -> 737 us (level)
  no operation moved by 1% of the time
where the time goes in v7:
time: 737 us
  Pallas kernels  736 us (100%)
    pallas_call x1, Pallas kernels, local_product(): pl.pallas_call(kernel, name='exchange_matmul', out_shape=(pltpu.VMEM((row...  736 us

profile of v7, /device:TPU:0, one launch (start us, length us, event | category | flops | bytes accessed | tf_op | source)
XLA Modules:
  0.0 737.1 jit_solution(71478110406229605)
XLA Ops:
  0.0 735.5 %exchange_matmul.1 = (bf16[256,5632]{1,0:T(8,128)(2,1)S(1)}, bf16[8,256,12288]{2,1,0:T(8,128)(2,1)}) custom-call(bf16[256,98304]{1,0:T(8,128)(2,1)} %a_ref.1, bf16[12288,5632]{1,0:T(8,128)(2,1)} %b_ref.1), custom_call_target="tpu_custom_call" | custom-call | flops 283467841536 | bytes 1107296256 | tf_op jit(solution)/shard_map/exchange_matmul/pallas_call | solution.py:237
  735.5 1.6 copy.4

commit v8 on v6

--- a/solution.py
+++ b/solution.py
@@ -13,9 +13,9 @@
 COLS = 512
 PIECE = 2048
 AHEAD = 2
-HELD = 12
+HELD = 16
 BURST = 2
-LAG1 = 4
+LAG1 = 5
 LAG2 = 3
 HELD2 = 4
 SUMS1, SUMS2 = HELD + LAG1 + 3, BURST * (HELD2 + LAG2 + 2)

time: 734 us -> 736 us (level)
  no operation moved by 1% of the time
where the time goes in v8:
time: 736 us
  Pallas kernels  734 us (100%)
    pallas_call x1, Pallas kernels, local_product(): pl.pallas_call(kernel, name='exchange_matmul', out_shape=(pltpu.VMEM((row...  734 us

profile of v8, /device:TPU:0, one launch (start us, length us, event | category | flops | bytes accessed | tf_op | source)
XLA Modules:
  0.0 735.7 jit_solution(15052352640080459266)
XLA Ops:
  0.0 734.1 %exchange_matmul.1 = (bf16[256,5632]{1,0:T(8,128)(2,1)S(1)}, bf16[8,256,12288]{2,1,0:T(8,128)(2,1)}) custom-call(bf16[256,98304]{1,0:T(8,128)(2,1)} %a_ref.1, bf16[12288,5632]{1,0:T(8,128)(2,1)} %b_ref.1), custom_call_target="tpu_custom_call" | custom-call | flops 283467841536 | bytes 1107296256 | tf_op jit(solution)/shard_map/exchange_matmul/pallas_call | solution.py:239
  734.1 1.6 copy.4
